TPU v7x, 32 devices: a whole 2x2x4 slice. The times are simulated.
32 devices in a mesh: grp: 2 (over y), mode: 8 (over z, x), node: 2 (over core).
Axes of the slice: x: 2, y: 2, z: 4, core: 2. Of those that a mesh axis runs over, the one named last changes fastest.
Arguments:
- mode_basis: float32 [4096, 4096], P('mode', 'node'), may hold values from -6 to 6
- mode_scales: float32 [4096], P('mode'), may hold values from 0.003 to 0.02
- mean_log: float32 [4096], P(('node', 'mode')), may hold values from -0.5 to 0.5
- sample_seeds: int32 [4096], P('grp'), parts along dimension 0, may hold values from 0 to 1073741823
Outputs:
- modulus: float32 [4096, 4096], P(('node', 'mode'), 'grp'), parts along dimension 1
- sample_means: float32 [4096], P('grp'), parts along dimension 0
There are 2 independent parts, one for each index of `grp`. A program takes and returns all parts, laid end to end along the dimension named above; an argument that names none is the same for every part. Nothing has to cross between parts.
All inputs are finite; a program needn't handle non-finite values.
Results may differ from a plain program's by a relative error of at most 0.00005.
Values sent between devices are 32-bit elements; how exact they have to be, the bound alone decides.
No kernel may reach another device: no remote copies, remote signals or barrier semaphores. Data moves between devices by JAX's collectives and lax.ppermute only.
A program may use at most 64 MiB of HBM per device.

v0:
```python
import math
import jax
import jax.numpy as jnp
from jax import lax
from jax.sharding import PartitionSpec as P


def scramble(seed_words, counter_words):
    mixed_word = seed_words * -1640531527 + counter_words * 668265261
    mixed_word = mixed_word ^ mixed_word >> 15 & 131071
    mixed_word = mixed_word * -2048144789
    mixed_word = mixed_word ^ mixed_word >> 13 & 524287
    mixed_word = mixed_word * -1028477387
    mixed_word = mixed_word ^ mixed_word >> 16 & 65535
    return mixed_word


def normals(sample_seeds, mode_start, mode_count):
    mode_ids = mode_start + jnp.arange(mode_count, dtype=jnp.int32)
    seed_words = sample_seeds[None, :]
    counter_words = (2 * mode_ids)[:, None]
    first_word = scramble(seed_words, counter_words)
    second_word = scramble(seed_words, counter_words + 1)
    first_unit = ((first_word & 16777215).astype(jnp.float32) + 0.5) * (1.0 / 16777216.0)
    second_unit = ((second_word & 16777215).astype(jnp.float32) + 0.5) * (1.0 / 16777216.0)
    radius = jnp.sqrt(-2.0 * jnp.log(first_unit))
    return radius * jnp.cos(2.0 * math.pi * second_unit)


def contract_all(all_modes, sample_seeds):
    mode_total = all_modes.shape[0]
    block_modes = min(512, mode_total)
    block_count = mode_total // block_modes
    start_total = jnp.zeros((all_modes.shape[1], sample_seeds.shape[0]), jnp.float32)

    def add_block(block, total):
        first_mode = (block * block_modes).astype(jnp.int32)
        rows = lax.dynamic_slice_in_dim(all_modes, first_mode, block_modes, 0)
        coeffs = normals(sample_seeds, first_mode, block_modes)
        return total + lax.dot_general(
            rows,
            coeffs,
            (((0,), (0,)), ((), ())),
            precision=lax.Precision.HIGHEST,
            preferred_element_type=jnp.float32,
        )

    return lax.fori_loop(0, block_count, add_block, start_total)


def on_device(mode_basis, mode_scales, mean_log, sample_seeds):
    own_rows = mean_log.shape[0]
    scaled = mode_scales[:, None] * mode_basis
    gathered = lax.all_to_all(scaled, "mode", split_axis=1, concat_axis=0, tiled=True)
    summed = contract_all(gathered, sample_seeds)
    modulus = jnp.exp(mean_log[:, None] + summed)
    totals = lax.psum(jnp.sum(modulus, axis=0), ("mode", "node"))
    node_count = own_rows * lax.axis_size("mode") * lax.axis_size("node")
    return (modulus, totals / node_count)


def solution(mesh):
    return jax.shard_map(
        on_device,
        mesh=mesh,
        in_specs=(P("mode", "node"), P("mode"), P(("node", "mode")), P("grp")),
        out_specs=(P(("node", "mode"), "grp"), P("grp")),
        check_vma=False,
    )
```

profile of v0, /device:TPU:0, one launch (start us, length us, event | category | flops | bytes accessed | tf_op | source)
XLA Modules:
  0.0 334.7 jit_solution(1991284625481277206)
XLA Ops:
  0.6 2.5 broadcast_multiply_fusion.1
  3.2 2.4 copy.9
  5.5 0.0 copy-start
  5.5 7.4 %all-to-all-start = ((f32[512,8,256]{2,0,1:T(8,128)}), f32[512,8,256]{2,0,1:T(8,128)}, u32[]{:S(2)}, u32[]{:S(2)}) async-start(f32[512,8,256]{2,0,1:T(8,128)} %bitcast.8), calls=%async_computation | async-start | bytes 8388608 | tf_op jit(solution)/shard_map/all_to_all | solution.py:54
  12.9 93.3 %all-to-all-done = f32[512,8,256]{2,0,1:T(8,128)} async-done(((f32[512,8,256]{2,0,1:T(8,128)}), f32[512,8,256]{2,0,1:T(8,128)}, u32[]{:S(2)}, u32[]{:S(2)}) %all-to-all-start) | async-done | bytes 4194336 | tf_op jit(solution)/shard_map/all_to_all | solution.py:54
  106.2 0.0 copy-done
  106.2 0.0 copy-start.1
  106.2 194.2 %while.16 = (s32[]{:T(128)}, f32[256,2048]{1,0:T(8,128)S(1)}, f32[4096,256]{1,0:T(8,128)}, s32[2048]{0:T(1024)S(1)}, s32[]{:T(128)}, /*index=5*/s32[]{:T(128)}, s32[]{:T(128)}, s32[]{:T(128)}) while((s32[]{:T(128)}, f32[256,2048]{1,0:T(8,128)S(1)}, f32[4096,256]{1,0:T(8,128)}, s32[2048]{0:T(1024)S(1)}, s32[]{:T(128)}, ...), condition=%wide.region_1.0_spmd.clone, body=%wide.region_0.0_spmd.clone.sunk | while | flops 3257930240 | bytes 4751509 | solution.py:48
  106.3 24.2 %fusion.75 = f32[256,2048]{1,0:T(8,128)S(1)} fusion(f32[256,2048]{1,0:T(8,128)S(1)} %get-tuple-element.179, s32[512]{0:T(512)S(1)} %get-tuple-element.168, s32[512]{0:T(512)S(1)} %get-tuple-element.169, s32[2048]{0:T(1024)S(1)} %broadcast_multiply_fusion.4, pred[]{:T(512)S(6)} %compare.3, f32[4096,256]{1,0:T(8,128)} %get-tuple-element.188, ...), kind=kOutput, calls=%fused_computation.36.clone.1 | convolution fusion | flops 3257925632 | bytes 4730885 | tf_op jit(solution)/shard_map/while/body/eval_jaxpr/dot_general | solution.py:40
  130.5 24.2 %fusion.75 = f32[256,2048]{1,0:T(8,128)S(1)} fusion(f32[256,2048]{1,0:T(8,128)S(1)} %get-tuple-element.179, s32[512]{0:T(512)S(1)} %get-tuple-element.168, s32[512]{0:T(512)S(1)} %get-tuple-element.169, s32[2048]{0:T(1024)S(1)} %broadcast_multiply_fusion.4, pred[]{:T(512)S(6)} %compare.3, f32[4096,256]{1,0:T(8,128)} %get-tuple-element.188, ...), kind=kOutput, calls=%fused_computation.36.clone.1 | convolution fusion | flops 3257925632 | bytes 4730885 | tf_op jit(solution)/shard_map/while/body/eval_jaxpr/dot_general | solution.py:40
  154.8 24.2 %fusion.75 = f32[256,2048]{1,0:T(8,128)S(1)} fusion(f32[256,2048]{1,0:T(8,128)S(1)} %get-tuple-element.179, s32[512]{0:T(512)S(1)} %get-tuple-element.168, s32[512]{0:T(512)S(1)} %get-tuple-element.169, s32[2048]{0:T(1024)S(1)} %broadcast_multiply_fusion.4, pred[]{:T(512)S(6)} %compare.3, f32[4096,256]{1,0:T(8,128)} %get-tuple-element.188, ...), kind=kOutput, calls=%fused_computation.36.clone.1 | convolution fusion | flops 3257925632 | bytes 4730885 | tf_op jit(solution)/shard_map/while/body/eval_jaxpr/dot_general | solution.py:40
  179.1 24.2 %fusion.75 = f32[256,2048]{1,0:T(8,128)S(1)} fusion(f32[256,2048]{1,0:T(8,128)S(1)} %get-tuple-element.179, s32[512]{0:T(512)S(1)} %get-tuple-element.168, s32[512]{0:T(512)S(1)} %get-tuple-element.169, s32[2048]{0:T(1024)S(1)} %broadcast_multiply_fusion.4, pred[]{:T(512)S(6)} %compare.3, f32[4096,256]{1,0:T(8,128)} %get-tuple-element.188, ...), kind=kOutput, calls=%fused_computation.36.clone.1 | convolution fusion | flops 3257925632 | bytes 4730885 | tf_op jit(solution)/shard_map/while/body/eval_jaxpr/dot_general | solution.py:40
  203.4 24.2 %fusion.75 = f32[256,2048]{1,0:T(8,128)S(1)} fusion(f32[256,2048]{1,0:T(8,128)S(1)} %get-tuple-element.179, s32[512]{0:T(512)S(1)} %get-tuple-element.168, s32[512]{0:T(512)S(1)} %get-tuple-element.169, s32[2048]{0:T(1024)S(1)} %broadcast_multiply_fusion.4, pred[]{:T(512)S(6)} %compare.3, f32[4096,256]{1,0:T(8,128)} %get-tuple-element.188, ...), kind=kOutput, calls=%fused_computation.36.clone.1 | convolution fusion | flops 3257925632 | bytes 4730885 | tf_op jit(solution)/shard_map/while/body/eval_jaxpr/dot_general | solution.py:40
  227.6 24.2 %fusion.75 = f32[256,2048]{1,0:T(8,128)S(1)} fusion(f32[256,2048]{1,0:T(8,128)S(1)} %get-tuple-element.179, s32[512]{0:T(512)S(1)} %get-tuple-element.168, s32[512]{0:T(512)S(1)} %get-tuple-element.169, s32[2048]{0:T(1024)S(1)} %broadcast_multiply_fusion.4, pred[]{:T(512)S(6)} %compare.3, f32[4096,256]{1,0:T(8,128)} %get-tuple-element.188, ...), kind=kOutput, calls=%fused_computation.36.clone.1 | convolution fusion | flops 3257925632 | bytes 4730885 | tf_op jit(solution)/shard_map/while/body/eval_jaxpr/dot_general | solution.py:40
  251.9 24.2 %fusion.75 = f32[256,2048]{1,0:T(8,128)S(1)} fusion(f32[256,2048]{1,0:T(8,128)S(1)} %get-tuple-element.179, s32[512]{0:T(512)S(1)} %get-tuple-element.168, s32[512]{0:T(512)S(1)} %get-tuple-element.169, s32[2048]{0:T(1024)S(1)} %broadcast_multiply_fusion.4, pred[]{:T(512)S(6)} %compare.3, f32[4096,256]{1,0:T(8,128)} %get-tuple-element.188, ...), kind=kOutput, calls=%fused_computation.36.clone.1 | convolution fusion | flops 3257925632 | bytes 4730885 | tf_op jit(solution)/shard_map/while/body/eval_jaxpr/dot_general | solution.py:40
  276.2 24.2 %fusion.75 = f32[256,2048]{1,0:T(8,128)S(1)} fusion(f32[256,2048]{1,0:T(8,128)S(1)} %get-tuple-element.179, s32[512]{0:T(512)S(1)} %get-tuple-element.168, s32[512]{0:T(512)S(1)} %get-tuple-element.169, s32[2048]{0:T(1024)S(1)} %broadcast_multiply_fusion.4, pred[]{:T(512)S(6)} %compare.3, f32[4096,256]{1,0:T(8,128)} %get-tuple-element.188, ...), kind=kOutput, calls=%fused_computation.36.clone.1 | convolution fusion | flops 3257925632 | bytes 4730885 | tf_op jit(solution)/shard_map/while/body/eval_jaxpr/dot_general | solution.py:40
  300.4 0.0 copy-done.1
  300.4 1.7 fusion.69
  302.1 32.0 %psum.7 = f32[2048]{0:T(1024)S(1)} all-reduce(f32[2048]{0:T(1024)S(1)} %get-tuple-element.137), channel_id=1, replica_groups=mesh['grp'=2,'mode'=8,'node'=2] {'mode','node'}, use_global_device_ids=true, to_apply=%region_3.0 | all-reduce | flops 2048 | bytes 16384 | tf_op jit(solution)/shard_map/psum | solution.py:57
  334.1 0.6 broadcast_multiply_fusion.2
  (17 shorter events, 0.1 us)
Async XLA Ops:
  5.5 100.7 %copy-start = (s32[2048]{0:T(1024)S(1)}, s32[2048]{0:T(1024)}, u32[]{:S(2)}) copy-start(s32[2048]{0:T(1024)} %param.9) | copy-start | bytes 24580
  5.5 100.7 %all-to-all-start = ((f32[512,8,256]{2,0,1:T(8,128)}), f32[512,8,256]{2,0,1:T(8,128)}, u32[]{:S(2)}, u32[]{:S(2)}) async-start(f32[512,8,256]{2,0,1:T(8,128)} %bitcast.8), calls=%async_computation | async-start | bytes 8388608 | tf_op jit(solution)/shard_map/all_to_all | solution.py:54
  106.2 194.2 %copy-start.1 = (f32[256]{0:T(256)S(1)}, f32[256]{0:T(256)}, u32[]{:S(2)}) copy-start(f32[256]{0:T(256)} %param.8) | copy-start | bytes 3076
where the time goes:
time: 335 us
  matrix products  194 us (58%)
  waiting for transfers between devices  93.3 us (28%)
  blocking collectives  32 us (10%)
  starting transfers between devices  7.41 us (2%)
  other arithmetic  4.88 us (1%)
    dot_general x8, matrix products, add_block(): lax.dot_general(rows, coeffs, (((0,), (0,)), ((), ())), precision=lax.Pre...  194 us
    all_to_all x1, waiting for transfers between devices, on_device(): lax.all_to_all(scaled, 'mode', split_axis=1, concat_axis=0, tiled=True)  93.3 us
    psum x1, blocking collectives, on_device(): totals = lax.psum(jnp.sum(modulus, axis=0), ('mode', 'node'))  32 us
    all_to_all x1, starting transfers between devices, on_device(): lax.all_to_all(scaled, 'mode', split_axis=1, concat_axis=0, tiled=True)  7.41 us
  transfers between devices with their start and end apart: 1, of which 1 were waited for; matrix products, arithmetic and copies ran while one was open for 0% of the time, Pallas kernels for 0%

commit v1 on v0

--- a/solution.py
+++ b/solution.py
@@ -54,7 +54,7 @@
     gathered = lax.all_to_all(scaled, "mode", split_axis=1, concat_axis=0, tiled=True)
     summed = contract_all(gathered, sample_seeds)
     modulus = jnp.exp(mean_log[:, None] + summed)
-    totals = lax.psum(jnp.sum(modulus, axis=0), ("mode", "node"))
+    totals = jnp.sum(lax.all_gather(jnp.sum(modulus, axis=0), ("mode", "node")), axis=0)
     node_count = own_rows * lax.axis_size("mode") * lax.axis_size("node")
     return (modulus, totals / node_count)
 

time: 335 us -> 323 us (0.964)
  blocking collectives: 32 us -> 19.8 us
    psum x1 -> x0, blocking collectives: 32 us -> none  [on_device(): totals = lax.psum(jnp.sum(modulus, axis=0), ('mode', 'node'))]
    all_gather x0 -> x1, blocking collectives: none -> 19.8 us  [on_device(): lax.all_gather(jnp.sum(modulus, axis=0), ('mode', 'node'))]
where the time goes in v1:
time: 323 us
  matrix products  194 us (60%)
  waiting for transfers between devices  93.3 us (29%)
  blocking collectives  19.8 us (6%)
  starting transfers between devices  7.41 us (2%)
  other arithmetic  4.9 us (2%)
    dot_general x8, matrix products, add_block(): lax.dot_general(rows, coeffs, (((0,), (0,)), ((), ())), precision=lax.Pre...  194 us
    all_to_all x1, waiting for transfers between devices, on_device(): lax.all_to_all(scaled, 'mode', split_axis=1, concat_axis=0, tiled=True)  93.3 us
    all_gather x1, blocking collectives, on_device(): lax.all_gather(jnp.sum(modulus, axis=0), ('mode', 'node'))  19.8 us
    all_to_all x1, starting transfers between devices, on_device(): lax.all_to_all(scaled, 'mode', split_axis=1, concat_axis=0, tiled=True)  7.41 us
  transfers between devices with their start and end apart: 1, of which 1 were waited for; matrix products, arithmetic and copies ran while one was open for 0% of the time, Pallas kernels for 0%

profile of v1, /device:TPU:0, one launch (start us, length us, event | category | flops | bytes accessed | tf_op | source)
XLA Modules:
  0.0 322.6 jit_solution(9304988573078148034)
XLA Ops:
  0.6 2.5 broadcast_multiply_fusion.1
  3.2 2.4 copy.11
  5.5 0.0 copy-start
  5.5 7.4 %all-to-all-start = ((f32[512,8,256]{2,0,1:T(8,128)}), f32[512,8,256]{2,0,1:T(8,128)}, u32[]{:S(2)}, u32[]{:S(2)}) async-start(f32[512,8,256]{2,0,1:T(8,128)} %bitcast.8), calls=%async_computation | async-start | bytes 8388608 | tf_op jit(solution)/shard_map/all_to_all | solution.py:54
  12.9 93.3 %all-to-all-done = f32[512,8,256]{2,0,1:T(8,128)} async-done(((f32[512,8,256]{2,0,1:T(8,128)}), f32[512,8,256]{2,0,1:T(8,128)}, u32[]{:S(2)}, u32[]{:S(2)}) %all-to-all-start) | async-done | bytes 4194336 | tf_op jit(solution)/shard_map/all_to_all | solution.py:54
  106.2 0.0 copy-done
  106.2 0.0 copy-start.1
  106.2 194.2 %while.16 = (s32[]{:T(128)}, f32[256,2048]{1,0:T(8,128)S(1)}, f32[4096,256]{1,0:T(8,128)}, s32[2048]{0:T(1024)S(1)}, s32[]{:T(128)}, /*index=5*/s32[]{:T(128)}, s32[]{:T(128)}, s32[]{:T(128)}) while((s32[]{:T(128)}, f32[256,2048]{1,0:T(8,128)S(1)}, f32[4096,256]{1,0:T(8,128)}, s32[2048]{0:T(1024)S(1)}, s32[]{:T(128)}, ...), condition=%wide.region_1.0_spmd.clone, body=%wide.region_0.0_spmd.clone.sunk | while | flops 3257930240 | bytes 4751509 | solution.py:48
  106.3 24.2 %fusion.75 = f32[256,2048]{1,0:T(8,128)S(1)} fusion(f32[256,2048]{1,0:T(8,128)S(1)} %get-tuple-element.179, s32[512]{0:T(512)S(1)} %get-tuple-element.168, s32[512]{0:T(512)S(1)} %get-tuple-element.169, s32[2048]{0:T(1024)S(1)} %broadcast_multiply_fusion.4, pred[]{:T(512)S(6)} %compare.3, f32[4096,256]{1,0:T(8,128)} %get-tuple-element.188, ...), kind=kOutput, calls=%fused_computation.36.clone.1 | convolution fusion | flops 3257925632 | bytes 4730885 | tf_op jit(solution)/shard_map/while/body/eval_jaxpr/dot_general | solution.py:40
  130.5 24.2 %fusion.75 = f32[256,2048]{1,0:T(8,128)S(1)} fusion(f32[256,2048]{1,0:T(8,128)S(1)} %get-tuple-element.179, s32[512]{0:T(512)S(1)} %get-tuple-element.168, s32[512]{0:T(512)S(1)} %get-tuple-element.169, s32[2048]{0:T(1024)S(1)} %broadcast_multiply_fusion.4, pred[]{:T(512)S(6)} %compare.3, f32[4096,256]{1,0:T(8,128)} %get-tuple-element.188, ...), kind=kOutput, calls=%fused_computation.36.clone.1 | convolution fusion | flops 3257925632 | bytes 4730885 | tf_op jit(solution)/shard_map/while/body/eval_jaxpr/dot_general | solution.py:40
  154.8 24.2 %fusion.75 = f32[256,2048]{1,0:T(8,128)S(1)} fusion(f32[256,2048]{1,0:T(8,128)S(1)} %get-tuple-element.179, s32[512]{0:T(512)S(1)} %get-tuple-element.168, s32[512]{0:T(512)S(1)} %get-tuple-element.169, s32[2048]{0:T(1024)S(1)} %broadcast_multiply_fusion.4, pred[]{:T(512)S(6)} %compare.3, f32[4096,256]{1,0:T(8,128)} %get-tuple-element.188, ...), kind=kOutput, calls=%fused_computation.36.clone.1 | convolution fusion | flops 3257925632 | bytes 4730885 | tf_op jit(solution)/shard_map/while/body/eval_jaxpr/dot_general | solution.py:40
  179.1 24.2 %fusion.75 = f32[256,2048]{1,0:T(8,128)S(1)} fusion(f32[256,2048]{1,0:T(8,128)S(1)} %get-tuple-element.179, s32[512]{0:T(512)S(1)} %get-tuple-element.168, s32[512]{0:T(512)S(1)} %get-tuple-element.169, s32[2048]{0:T(1024)S(1)} %broadcast_multiply_fusion.4, pred[]{:T(512)S(6)} %compare.3, f32[4096,256]{1,0:T(8,128)} %get-tuple-element.188, ...), kind=kOutput, calls=%fused_computation.36.clone.1 | convolution fusion | flops 3257925632 | bytes 4730885 | tf_op jit(solution)/shard_map/while/body/eval_jaxpr/dot_general | solution.py:40
  203.4 24.2 %fusion.75 = f32[256,2048]{1,0:T(8,128)S(1)} fusion(f32[256,2048]{1,0:T(8,128)S(1)} %get-tuple-element.179, s32[512]{0:T(512)S(1)} %get-tuple-element.168, s32[512]{0:T(512)S(1)} %get-tuple-element.169, s32[2048]{0:T(1024)S(1)} %broadcast_multiply_fusion.4, pred[]{:T(512)S(6)} %compare.3, f32[4096,256]{1,0:T(8,128)} %get-tuple-element.188, ...), kind=kOutput, calls=%fused_computation.36.clone.1 | convolution fusion | flops 3257925632 | bytes 4730885 | tf_op jit(solution)/shard_map/while/body/eval_jaxpr/dot_general | solution.py:40
  227.6 24.2 %fusion.75 = f32[256,2048]{1,0:T(8,128)S(1)} fusion(f32[256,2048]{1,0:T(8,128)S(1)} %get-tuple-element.179, s32[512]{0:T(512)S(1)} %get-tuple-element.168, s32[512]{0:T(512)S(1)} %get-tuple-element.169, s32[2048]{0:T(1024)S(1)} %broadcast_multiply_fusion.4, pred[]{:T(512)S(6)} %compare.3, f32[4096,256]{1,0:T(8,128)} %get-tuple-element.188, ...), kind=kOutput, calls=%fused_computation.36.clone.1 | convolution fusion | flops 3257925632 | bytes 4730885 | tf_op jit(solution)/shard_map/while/body/eval_jaxpr/dot_general | solution.py:40
  251.9 24.2 %fusion.75 = f32[256,2048]{1,0:T(8,128)S(1)} fusion(f32[256,2048]{1,0:T(8,128)S(1)} %get-tuple-element.179, s32[512]{0:T(512)S(1)} %get-tuple-element.168, s32[512]{0:T(512)S(1)} %get-tuple-element.169, s32[2048]{0:T(1024)S(1)} %broadcast_multiply_fusion.4, pred[]{:T(512)S(6)} %compare.3, f32[4096,256]{1,0:T(8,128)} %get-tuple-element.188, ...), kind=kOutput, calls=%fused_computation.36.clone.1 | convolution fusion | flops 3257925632 | bytes 4730885 | tf_op jit(solution)/shard_map/while/body/eval_jaxpr/dot_general | solution.py:40
  276.2 24.2 %fusion.75 = f32[256,2048]{1,0:T(8,128)S(1)} fusion(f32[256,2048]{1,0:T(8,128)S(1)} %get-tuple-element.179, s32[512]{0:T(512)S(1)} %get-tuple-element.168, s32[512]{0:T(512)S(1)} %get-tuple-element.169, s32[2048]{0:T(1024)S(1)} %broadcast_multiply_fusion.4, pred[]{:T(512)S(6)} %compare.3, f32[4096,256]{1,0:T(8,128)} %get-tuple-element.188, ...), kind=kOutput, calls=%fused_computation.36.clone.1 | convolution fusion | flops 3257925632 | bytes 4730885 | tf_op jit(solution)/shard_map/while/body/eval_jaxpr/dot_general | solution.py:40
  300.4 0.0 copy-done.1
  300.4 1.7 fusion.69
  302.1 19.8 %all-gather = f32[32768]{0:T(1024)S(1)} all-gather(f32[2048]{0:T(1024)S(1)} %get-tuple-element.137), channel_id=2, replica_groups=mesh['grp'=2,'mode'=8,'node'=2] {'mode','node'}, dimensions={0}, use_global_device_ids=true | all-gather | bytes 139264 | tf_op jit(solution)/shard_map/all_gather | solution.py:57
  322.0 0.6 broadcast_multiply_fusion.2
  (19 shorter events, 0.1 us)
Async XLA Ops:
  5.5 100.7 %copy-start = (s32[2048]{0:T(1024)S(1)}, s32[2048]{0:T(1024)}, u32[]{:S(2)}) copy-start(s32[2048]{0:T(1024)} %param.9) | copy-start | bytes 24580
  5.5 100.7 %all-to-all-start = ((f32[512,8,256]{2,0,1:T(8,128)}), f32[512,8,256]{2,0,1:T(8,128)}, u32[]{:S(2)}, u32[]{:S(2)}) async-start(f32[512,8,256]{2,0,1:T(8,128)} %bitcast.8), calls=%async_computation | async-start | bytes 8388608 | tf_op jit(solution)/shard_map/all_to_all | solution.py:54
  106.2 194.2 %copy-start.1 = (f32[256]{0:T(256)S(1)}, f32[256]{0:T(256)}, u32[]{:S(2)}) copy-start(f32[256]{0:T(256)} %param.8) | copy-start | bytes 3076
